TPU v7x, 32 devices: a whole 2x2x4 slice. The times are simulated.
32 devices in a mesh: layer: 8 (over y, x, core), row: 4 (over z).
Axes of the slice: x: 2, y: 2, z: 4, core: 2. Of those that a mesh axis runs over, the one named last changes fastest.
Arguments:
- magnet: float32 [3, 8, 1024, 1024], P(None, 'layer', 'row'), may hold values from -1 to 1, as said below
- saturation: float32 [8], P('layer'), may hold values from 0.5 to 2
- stiffness: float32 [8], P('layer'), may hold values from 0.1 to 0.4
- damping: float32 [8], P('layer'), may hold values from 0.02 to 0.5
- interface_sign: int32 [8, 2], P('layer'), may hold values from -1 to 1, as said below
Outputs:
- torque: float32 [3, 8, 1024, 1024], P(None, 'layer', 'row')
Inputs may be any that keep to these rules, and one draw needn't show every extreme that they name: `magnet`: the three components of every cell form a unit vector. Every entry is -1 or 1; interface_sign[l, 1] equals interface_sign[l + 1, 0], the sign of the interface between layers l and l + 1; interface_sign[0, 0] and interface_sign[7, 1] belong to no interface.
All inputs are finite; a program needn't handle non-finite values.
Results may differ from a plain program's by a relative error of at most 0.0003.
Values sent between devices are 32-bit elements; how exact they have to be, the bound alone decides.
A program may use at most 128 MiB of HBM per device.

v0:
```python
import math

import jax
import jax.numpy as jnp
from jax import lax
from jax.sharding import PartitionSpec as P

NX = 1024
NY = 1024


THICKNESS = 1.0
LAYER_PITCH = 1.5
RKKY_STRENGTH = 0.8
HIGHEST = lax.Precision.HIGHEST


def with_halo(block, sides, width, periodic):
    for axis, dim in sides:
        count = lax.axis_size(axis)
        forward = [(i, i + 1) for i in range(count - 1)]
        if periodic:
            forward.append((count - 1, 0))
        backward = [(target, source) for source, target in forward]
        low = lax.ppermute(
            lax.slice_in_dim(block, block.shape[dim] - width, None, axis=dim), axis, forward
        )
        high = lax.ppermute(lax.slice_in_dim(block, 0, width, axis=dim), axis, backward)
        block = jnp.concatenate([low, block, high], axis=dim)
    return block


def spin_tables(count_one, count_two, modulus, orient):
    first_ids = jnp.arange(count_one, dtype=jnp.int32)
    second_ids = jnp.arange(count_two, dtype=jnp.int32)
    phase_index = first_ids[:, None] * second_ids[None, :] % modulus
    angles = 2.0 * math.pi / modulus * phase_index.astype(jnp.float32)
    return (jnp.cos(angles), orient * jnp.sin(angles))


def complex_apply(table_cos, table_sin, real_in, imag_in, form):
    real_out = jnp.einsum(form, table_cos, real_in, precision=HIGHEST) - jnp.einsum(
        form, table_sin, imag_in, precision=HIGHEST
    )
    imag_out = jnp.einsum(form, table_cos, imag_in, precision=HIGHEST) + jnp.einsum(
        form, table_sin, real_in, precision=HIGHEST
    )
    return (real_out, imag_out)


def transform(real_in, imag_in, along_dim, orient, forward):
    full_shape = real_in.shape
    length = full_shape[along_dim]
    inner_size = min(128, length)
    outer_size = length // inner_size
    split_shape = full_shape[:along_dim] + (outer_size, inner_size) + full_shape[along_dim + 1 :]
    real_in = real_in.reshape(split_shape)
    imag_in = imag_in.reshape(split_shape)
    leading = "mnop"[:along_dim]
    trailing = "qrst"[: len(full_shape) - along_dim - 1]
    twist_cos, twist_sin = spin_tables(outer_size, inner_size, length, orient)
    twist_cos = twist_cos.reshape((outer_size, inner_size) + (1,) * len(trailing))
    twist_sin = twist_sin.reshape((outer_size, inner_size) + (1,) * len(trailing))
    outer_cos, outer_sin = spin_tables(outer_size, outer_size, outer_size, orient)
    inner_cos, inner_sin = spin_tables(inner_size, inner_size, inner_size, orient)
    if forward:
        real_mid, imag_mid = complex_apply(
            outer_cos,
            outer_sin,
            real_in,
            imag_in,
            "ka," + leading + "ab" + trailing + "->" + leading + "kb" + trailing,
        )
        real_tw = real_mid * twist_cos - imag_mid * twist_sin
        imag_tw = imag_mid * twist_cos + real_mid * twist_sin
        real_out, imag_out = complex_apply(
            inner_cos,
            inner_sin,
            real_tw,
            imag_tw,
            "bj," + leading + "kb" + trailing + "->" + leading + "kj" + trailing,
        )
    else:
        real_mid, imag_mid = complex_apply(
            inner_cos,
            inner_sin,
            real_in,
            imag_in,
            "bj," + leading + "ab" + trailing + "->" + leading + "aj" + trailing,
        )
        real_tw = real_mid * twist_cos - imag_mid * twist_sin
        imag_tw = imag_mid * twist_cos + real_mid * twist_sin
        real_out, imag_out = complex_apply(
            outer_cos,
            outer_sin,
            real_tw,
            imag_tw,
            "ak," + leading + "aj" + trailing + "->" + leading + "kj" + trailing,
        )
    return (real_out.reshape(full_shape), imag_out.reshape(full_shape))


def wave_numbers(start_at, how_many, length):
    stored = start_at + jnp.arange(how_many, dtype=jnp.int32)
    inner_size = min(128, length)
    outer_size = length // inner_size
    position = stored // inner_size + outer_size * (stored % inner_size)
    position = jnp.where(position < length // 2, position, position - length)
    return 2.0 * math.pi / length * position.astype(jnp.float32)


def plane_factors(wave_y, wave_x):
    square = wave_y[:, None] * wave_y[:, None] + wave_x[None, :] * wave_x[None, :]
    anchor = square == 0.0
    wave_norm = jnp.sqrt(jnp.where(anchor, 1.0, square))
    unit_x = jnp.where(anchor, 0.0, wave_x[None, :] / wave_norm)
    unit_y = jnp.where(anchor, 0.0, wave_y[:, None] / wave_norm)
    self_z = jnp.where(anchor, 1.0, -jnp.expm1(-THICKNESS * wave_norm) / (THICKNESS * wave_norm))
    form_factor = jnp.where(
        anchor, 0.0, jnp.expm1(-THICKNESS * wave_norm) ** 2 / (2.0 * THICKNESS * wave_norm)
    )
    return (unit_x, unit_y, wave_norm, self_z, form_factor)


def forward_x(source, blocks, block_width):
    real_out, imag_out = transform(source, jnp.zeros_like(source), 3, -1.0, True)
    block_shape = source.shape[:3] + (blocks, 1, block_width)
    joined = jnp.concatenate([real_out.reshape(block_shape), imag_out.reshape(block_shape)], axis=4)
    return joined.reshape(source.shape[:3] + (blocks, 2 * block_width))


def forward_y(gathered):
    block_width = gathered.shape[4] // 2
    halves = gathered.reshape(gathered.shape[:3] + (2, block_width))
    real_out, imag_out = transform(halves[:, :, :, 0], halves[:, :, :, 1], 2, -1.0, True)
    return jnp.stack([real_out, imag_out], axis=3)


def inverse_y(spectra):
    length = spectra.shape[2]
    real_out, imag_out = transform(spectra[:, :, :, 0], spectra[:, :, :, 1], 2, 1.0, False)
    filled = jnp.stack([real_out, imag_out], axis=3) / length
    return filled.reshape(filled.shape[:3] + (1, 2 * filled.shape[4]))


def inverse_x(received):
    blocks = received.shape[3]
    block_width = received.shape[4] // 2
    split_view = received.reshape(received.shape[:3] + (blocks, 2, block_width))
    length = blocks * block_width
    real_part = split_view[:, :, :, :, 0].reshape(received.shape[:3] + (length,))
    imag_part = split_view[:, :, :, :, 1].reshape(received.shape[:3] + (length,))
    real_out, imag_out = transform(real_part, imag_part, 3, 1.0, False)
    return real_out / length


def contract(weight, values):
    return jnp.einsum("tmyx,myx->tyx", weight, values, precision=HIGHEST)


def couple(target_ids, source_ids, sources, wave_norm, form_factor):
    layer_gap = target_ids[:, None] - source_ids[None, :]
    distance = jnp.abs(layer_gap).astype(jnp.float32)[:, :, None, None]
    gap_sign = jnp.sign(layer_gap).astype(jnp.float32)[:, :, None, None]
    weight = jnp.where(
        (layer_gap == 0)[:, :, None, None],
        0.0,
        form_factor[None, None]
        * jnp.exp(-wave_norm[None, None] * (LAYER_PITCH * distance - THICKNESS)),
    )
    signed = weight * gap_sign
    along_real = sources[0, :, :, 0]
    along_imag = sources[0, :, :, 1]
    normal_real = sources[1, :, :, 0]
    normal_imag = sources[1, :, :, 1]
    psi_real = contract(weight, along_real) + contract(signed, normal_imag)
    psi_imag = contract(weight, along_imag) - contract(signed, normal_real)
    chi_real = contract(weight, normal_real) - contract(signed, along_imag)
    chi_imag = contract(weight, normal_imag) + contract(signed, along_real)
    return jnp.stack(
        [jnp.stack([psi_real, psi_imag], axis=2), jnp.stack([chi_real, chi_imag], axis=2)], axis=0
    )


def cross_product(vector_one, vector_two):
    return jnp.stack(
        [
            vector_one[1] * vector_two[2] - vector_one[2] * vector_two[1],
            vector_one[2] * vector_two[0] - vector_one[0] * vector_two[2],
            vector_one[0] * vector_two[1] - vector_one[1] * vector_two[0],
        ]
    )


def on_device(magnet, saturation, stiffness, damping, interface_sign):
    blocks = lax.axis_size("row")
    block_width = NX // blocks
    source = magnet * saturation[None, :, None, None]
    along_rows = forward_x(source, blocks, block_width)
    spectra = forward_y(lax.all_to_all(along_rows, "row", split_axis=3, concat_axis=2, tiled=True))
    row_at = lax.axis_index("row")
    wave_x = wave_numbers(row_at * block_width, block_width, NX)
    wave_y = wave_numbers(0, NY, NY)
    unit_x, unit_y, wave_norm, self_z, form_factor = plane_factors(wave_y, wave_x)
    along_wave = unit_x[:, None] * spectra[0] + unit_y[:, None] * spectra[1]
    normal = spectra[2]
    sources = jnp.stack([along_wave, normal])
    regrouped = lax.all_to_all(sources, "layer", split_axis=2, concat_axis=1, tiled=True)
    band_rows = regrouped.shape[2]
    band_y = wave_numbers(lax.axis_index("layer") * band_rows, band_rows, NY)
    band_factors = plane_factors(band_y, wave_x)
    all_ids = jnp.arange(regrouped.shape[1], dtype=jnp.int32)
    mixed_band = couple(all_ids, all_ids, regrouped, band_factors[2], band_factors[4])
    coupled = lax.all_to_all(mixed_band, "layer", split_axis=1, concat_axis=2, tiled=True)
    psi_total = coupled[0] + (1.0 - self_z)[:, None] * along_wave
    chi_total = coupled[1] + self_z[:, None] * normal
    field_spectra = jnp.stack(
        [-unit_x[:, None] * psi_total, -unit_y[:, None] * psi_total, -chi_total]
    )
    demag_field = inverse_x(
        lax.all_to_all(inverse_y(field_spectra), "row", split_axis=2, concat_axis=3, tiled=True)
    )
    with_rims = with_halo(magnet, (("row", 2),), 1, True)
    laplace = (
        with_rims[:, :, 2:]
        + with_rims[:, :, :-2]
        + jnp.roll(magnet, 1, 3)
        + jnp.roll(magnet, -1, 3)
        - 4.0 * magnet
    )
    exchange_field = stiffness[None, :, None, None] * laplace
    stacked = with_halo(magnet, (("layer", 1),), 1, False)
    layer_below = stacked[:, :-2]
    layer_above = stacked[:, 2:]
    sign_value = interface_sign.astype(jnp.float32)
    rkky_field = RKKY_STRENGTH * (
        sign_value[None, :, 0, None, None] * layer_below
        + sign_value[None, :, 1, None, None] * layer_above
    )
    total_field = demag_field + exchange_field + rkky_field
    precess = cross_product(magnet, total_field)
    relax_term = cross_product(magnet, precess)
    damping_now = damping[None, :, None, None]
    return -(precess + damping_now * relax_term) / (1.0 + damping_now * damping_now)


def solution(mesh):
    in_specs = (P(None, "layer", "row", None), P("layer"), P("layer"), P("layer"), P("layer", None))
    out_specs = P(None, "layer", "row", None)
    return jax.shard_map(
        on_device, mesh=mesh, in_specs=in_specs, out_specs=out_specs, check_vma=False
    )
```

profile of v0, /device:TPU:2, one launch (start us, length us, event | category | flops | bytes accessed | tf_op | source)
XLA Modules:
  0.0 686.3 jit_solution(11038566050253650016)
XLA Ops:
  10.3 4.0 fusion.23
  14.4 3.6 fusion.48
  21.6 3.6 fusion.59
  25.2 16.5 %fusion.62 = f32[3,256,8,128]{1,3,2,0:T(8,128)S(1)} fusion(f32[3,256,8,128]{1,3,2,0:T(8,128)S(1)} %fusion.46, f32[3,256,8,128]{3,2,1,0:T(8,128)S(1)} %get-tuple-element.30), kind=kOutput, calls=%fused_computation.104 | convolution fusion | flops 1208991744 | bytes 9437184 | tf_op jit(solution)/shard_map/bj,mnokb->mnokj/dot_general | solution.py:45
  45.7 5.2 all-to-all-start
  51.2 3.7 fusion.100
  54.9 134.5 %all-to-all-done = f32[3,1,256,4,512]{2,4,0,1,3:T(8,128)} async-done(((f32[3,1,256,4,512]{2,4,0,1,3:T(8,128)}), f32[3,1,256,4,512]{2,4,0,1,3:T(8,128)}, u32[]{:S(2)}, u32[]{:S(2)}) %all-to-all-start) | async-done | bytes 6291488 | tf_op jit(solution)/shard_map/all_to_all | solution.py:200
  189.4 6.6 copy.285
  196.0 8.2 %reshape.967 = f32[3,1,1024,2,256]{4,3,2,0,1:T(2,128)} reshape(f32[3,1,4,256,1,512]{5,3,2,0,4,1:T(8,128)} %copy.285) | data formatting | bytes 12582912 | tf_op jit(solution)/shard_map/reshape | solution.py:134
  204.2 11.7 %fusion.371 = (f32[3,1,1024,1,256]{4,3,2,0,1:T(1,128)S(1)}, f32[3,1,1024,1,256]{4,3,2,0,1:T(1,128)}) fusion(f32[3,1,1024,2,256]{4,3,2,0,1:T(2,128)} %reshape.967), kind=kLoop, calls=%fused_computation.423 | loop fusion | bytes 12582912 | tf_op jit(solution)/shard_map/slice | solution.py:135
  217.9 4.7 fusion.40
  222.6 5.2 fusion.38
  228.1 5.0 fusion.71
  233.1 5.9 fusion.19
  239.0 4.1 fusion.30
  243.2 4.2 fusion.32
  247.3 4.5 fusion.68
  251.8 4.2 fusion.65
  258.2 5.2 copy.304
  263.5 5.4 all-to-all-start.1
  269.4 47.2 %all-to-all-done.1 = f32[2,1,1024,2,256]{4,0,3,1,2:T(2,128)} async-done(((f32[2,1,1024,2,256]{4,0,3,1,2:T(2,128)}), f32[2,1,1024,2,256]{4,0,3,1,2:T(2,128)}, u32[]{:S(2)}, u32[]{:S(2)}) %all-to-all-start.1) | async-done | bytes 4194336 | tf_op jit(solution)/shard_map/all_to_all | solution.py:208
  316.5 6.3 fusion.373
  323.3 12.2 %multiply_reduce_fusion.5 = (f32[128,256,8]{1,0,2:T(8,128)S(1)}, f32[128,256,8]{1,0,2:T(8,128)S(1)}, f32[128,256,8]{1,0,2:T(8,128)S(1)}, f32[128,256,8]{1,0,2:T(...) fusion(f32[128,256,8]{1,0,2:T(8,128)S(1)} %bitcast.368, ...), kind=kLoop, calls=%fused_computation.5 | loop fusion | flops 39845888 | bytes 12845632 | tf_op jit(solution)/shard_map/tmyx,myx->tyx/dot_general | solution.py:158
  338.9 6.1 all-to-all-start.2
  345.1 47.5 %all-to-all-done.2 = f32[2,8,128,2,256]{4,2,3,0,1:T(8,128)} async-done(((f32[2,8,128,2,256]{4,2,3,0,1:T(8,128)}), f32[2,8,128,2,256]{4,2,3,0,1:T(8,128)}, u32[]{:S(2)}, u32[]{:S(2)}) %all-to-all-start.2) | async-done | bytes 4194336 | tf_op jit(solution)/shard_map/all_to_all | solution.py:214
  400.9 5.2 fusion.125
  406.1 5.8 fusion.127
  411.9 5.4 convolution_add_fusion.1
  417.3 7.6 %fusion.15 = (f32[3,8,128,256]{2,3,1,0:T(8,128)}, f32[3,8,128,256]{2,3,1,0:T(8,128)}) fusion(f32[3,8,256,128]{3,2,1,0:T(8,128)S(1)} %convolution_add_fusion.1, f32[8,128]{1,0:T(8,128)S(1)} %fusion.206, f32[8,128]{1,0:T(8,128)S(1)} %get-tuple-element.67, f32[3,8,256,128]{3,2,1,0:T(8,128)S(1)} %fusion.127, f32[3,8,128,256]{3,2,1,0:T(8,128)S(1)} %bitcast.343), kind=kOutput, calls=%fused_computation.39 | convolution fusion | flops 1213693952 | bytes 15736832 | tf_op jit(solution)/shard_map/bj,mnabq->mnajq/dot_general | solution.py:42
  427.5 4.4 fusion.189
  431.9 3.7 copy.315
  435.7 5.1 fusion.187
  452.4 6.5 copy.320
  458.9 16.3 %copy.321 = f32[3,1,1024,1,512]{4,3,1,0,2:T(1,128)} copy(f32[3,1,1024,1,512]{2,4,0,3,1:T(8,128)} %bitcast.356) | data formatting | bytes 12582912 | tf_op jit(solution)/shard_map/div | solution.py:142
  475.3 5.5 all-to-all-start.3
  487.0 3.8 collective-permute-start
  493.0 3.9 fusion.374
  497.5 122.3 %all-to-all-done.3 = f32[3,1,1024,1,512]{4,3,1,0,2:T(1,128)} async-done(((f32[3,1,1024,1,512]{4,3,1,0,2:T(1,128)}), f32[3,1,1024,1,512]{4,3,1,0,2:T(1,128)}, u32[]{:S(2)}, u32[]{:S(2)}) %all-to-all-start.3) | async-done | bytes 6291488 | tf_op jit(solution)/shard_map/all_to_all | solution.py:221
  619.8 6.2 copy.322
  626.0 6.5 copy.323
  636.1 5.4 fusion.123
  641.4 5.4 fusion.121
  646.8 5.4 convolution_subtract_fusion
  652.2 5.5 multiply_subtract_fusion
  657.8 4.7 fusion.26
  662.5 6.4 multiply_bitcast_fusion
  668.9 4.6 div.134
  673.5 8.5 %fusion.11 = f32[3,1,256,1024]{3,2,1,0:T(8,128)S(1)} fusion(f32[3,1,256,1024]{3,2,1,0:T(8,128)S(1)} %copy-done.1, f32[3,1,1,1024]{3,2,1,0:T(1,128)} %collective-permute-done.1, f32[3,1,1,1024]{3,2,1,0:T(1,128)} %collective-permute-done, f32[3,1,256,1023]{3,2,1,0:T(8,128)} %get-tuple-element.49, f32[3,1,256,1]{3,2,1,0:T(8,128)} %get-tuple-element.51, ...), kind=kLoop, calls=%fused_computation.30 | loop fusion | flops 12582912 | bytes 22044684 | tf_op jit(solution)/shard_map/add | solution.py:240
  (92 shorter events, 63.9 us)
Async XLA Ops:
  0.1 6.1 copy-start
  45.7 143.7 %all-to-all-start = ((f32[3,1,256,4,512]{2,4,0,1,3:T(8,128)}), f32[3,1,256,4,512]{2,4,0,1,3:T(8,128)}, u32[]{:S(2)}, u32[]{:S(2)}) async-start(f32[3,1,256,4,512]{2,4,0,1,3:T(8,128)} %copy.284), calls=%async_computation | async-start | bytes 12582912 | tf_op jit(solution)/shard_map/all_to_all | solution.py:200
  251.8 4.2 copy-start.7
  251.8 4.2 copy-start.8
  256.6 1.3 copy-start.3
  263.5 53.1 %all-to-all-start.1 = ((f32[2,1,1024,2,256]{4,0,3,1,2:T(2,128)}), f32[2,1,1024,2,256]{4,0,3,1,2:T(2,128)}, u32[]{:S(2)}, u32[]{:S(2)}) async-start(f32[2,1,1024,2,256]{4,0,3,1,2:T(2,128)} %copy.304), calls=%async_computation.1 | async-start | bytes 8388608 | tf_op jit(solution)/shard_map/all_to_all | solution.py:208
  338.9 53.7 %all-to-all-start.2 = ((f32[2,8,128,2,256]{4,2,3,0,1:T(8,128)}), f32[2,8,128,2,256]{4,2,3,0,1:T(8,128)}, u32[]{:S(2)}, u32[]{:S(2)}) async-start(f32[2,8,128,2,256]{4,2,3,0,1:T(8,128)} %pad_maximum_fusion.3), calls=%async_computation.2 | async-start | bytes 8388608 | tf_op jit(solution)/shard_map/all_to_all | solution.py:214
  395.3 1.2 copy-start.6
  396.5 1.6 copy-start.4
  396.5 1.9 copy-start.9
  396.5 2.2 copy-start.10
  396.5 2.5 copy-start.11
  435.6 5.1 copy-start.2
  435.7 5.1 copy-start.5
  475.3 5.5 copy-start.1
  475.3 15.5 %copy-start.12 = (s32[1,2]{1,0:T(1,128)S(1)}, s32[1,2]{1,0:T(1,128)}, u32[]{:S(2)}) copy-start(s32[1,2]{1,0:T(1,128)} %param.9) | copy-start | bytes 28
  475.3 144.6 %all-to-all-start.3 = ((f32[3,1,1024,1,512]{4,3,1,0,2:T(1,128)}), f32[3,1,1024,1,512]{4,3,1,0,2:T(1,128)}, u32[]{:S(2)}, u32[]{:S(2)}) async-start(f32[3,1,1024,1,512]{4,3,1,0,2:T(1,128)} %copy.321), calls=%async_computation.3 | async-start | bytes 12582912 | tf_op jit(solution)/shard_map/all_to_all | solution.py:221
  480.8 192.7 %collective-permute-start.2 = (f32[3,1,256,1024]{3,2,1,0:T(8,128)S(1)}, f32[3,1,256,1024]{3,2,1,0:T(8,128)}, u32[]{:S(2)}, u32[]{:S(2)}) collective-permute-start(f32[3,1,256,1024]{3,2,1,0:T(8,128)S(1)} %copy-done.1), channel_id=1, source_target_pairs={{0,4},{4,8},{8,12},{12,16},{16,20},{20,24},{24,28},{1,5},{5,9},{9,... | collective-permute-start | bytes 9437192 | tf_op jit(solution)/shard_map/ppermute | solution.py:25
  482.8 190.7 %collective-permute-start.3 = (f32[3,1,256,1024]{3,2,1,0:T(8,128)S(1)}, f32[3,1,256,1024]{3,2,1,0:T(8,128)}, u32[]{:S(2)}, u32[]{:S(2)}) collective-permute-start(f32[3,1,256,1024]{3,2,1,0:T(8,128)S(1)} %copy-done.1), channel_id=1, source_target_pairs={{4,0},{8,4},{12,8},{16,12},{20,16},{24,20},{28,24},{5,1},{9,5},{13... | collective-permute-start | bytes 9437192 | tf_op jit(solution)/shard_map/ppermute | solution.py:28
  487.0 186.5 %collective-permute-start = (f32[3,1,1,1024]{3,2,1,0:T(1,128)}, f32[3,1,1,1024]{3,2,1,0:T(1,128)}, u32[]{:S(2)}, u32[]{:S(2)}) collective-permute-start(f32[3,1,1,1024]{3,2,1,0:T(1,128)} %get-tuple-element.52), channel_id=1, source_target_pairs={{1,0},{2,1},{3,2},{0,3},{5,4},{6,5},{7,6},{4,7},{9,8},{10,9},{11,1... | collective-permute-start | bytes 36872 | tf_op jit(solution)/shard_map/ppermute | solution.py:28
  490.8 182.7 %collective-permute-start.1 = (f32[3,1,1,1024]{3,2,1,0:T(1,128)}, f32[3,1,1,1024]{3,2,1,0:T(1,128)}, u32[]{:S(2)}, u32[]{:S(2)}) collective-permute-start(f32[3,1,1,1024]{3,2,1,0:T(1,128)} %get-tuple-element.53), channel_id=1, source_target_pairs={{0,1},{1,2},{2,3},{3,0},{4,5},{5,6},{6,7},{7,4},{8,9},{9,10},{10,1... | collective-permute-start | bytes 36872 | tf_op jit(solution)/shard_map/ppermute | solution.py:25
where the time goes:
time: 696 us; the launch traced here: 686 us
  waiting for transfers between devices  351 us (50%)
  matrix products  150 us (22%)
  local copies, waits for them, and re-layouts  112 us (16%)
  other arithmetic  38.5 us (6%)
  starting transfers between devices  31.6 us (5%)
    all_to_all x1, waiting for transfers between devices, on_device(): lax.all_to_all(along_rows, 'row', split_axis=3, concat_axis=2, tiled=True)  134 us
    all_to_all x1, waiting for transfers between devices, on_device(): lax.all_to_all(inverse_y(field_spectra), 'row', split_axis=2, concat_axis...  122 us
    all_to_all x1, waiting for transfers between devices, on_device(): lax.all_to_all(mixed_band, 'layer', split_axis=1, concat_axis=2, tiled=True)  47.5 us
    all_to_all x1, waiting for transfers between devices, on_device(): lax.all_to_all(sources, 'layer', split_axis=2, concat_axis=1, tiled=True)  47.2 us
    dot_general x7, matrix products, complex_apply(): jnp.einsum(form, table_sin, real_in, precision=HIGHEST)  45 us
    dot_general x8, matrix products, complex_apply(): jnp.einsum(form, table_cos, real_in, precision=HIGHEST)  37.9 us
    dot_general x8, matrix products, complex_apply(): jnp.einsum(form, table_sin, imag_in, precision=HIGHEST)  36 us
    dot_general x7, matrix products, complex_apply(): jnp.einsum(form, table_cos, imag_in, precision=HIGHEST)  31.3 us
  transfers between devices with their start and end apart: 8, of which 4 were waited for; matrix products, arithmetic and copies ran while one was open for 9% of the time, Pallas kernels for 0%

commit v1 on v0

v1 whole, which is shorter than its diff:
```python
import functools
import math

import jax
import jax.numpy as jnp
import numpy as np
from jax import lax
from jax.experimental import pallas as pl
from jax.experimental.pallas import tpu as pltpu
from jax.sharding import PartitionSpec as P

THICKNESS = 1.0
LAYER_PITCH = 1.5
RKKY_STRENGTH = 0.8
HIGH = lax.Precision.HIGH
LANES = 128


def angle_pair(phase):
    return np.cos(phase).astype(np.float32), np.sin(phase).astype(np.float32)


def turn(first, second, modulus):
    return 2.0 * math.pi / modulus * (np.outer(first, second) % modulus)


def outer_cosine(angle_one, angle_two):
    cos_one, sin_one = angle_pair(angle_one)
    cos_two, sin_two = angle_pair(angle_two)
    table = cos_one[:, None] * jnp.asarray(cos_two)[None] - sin_one[:, None] * jnp.asarray(sin_two)[None]
    return table.reshape(-1, table.shape[2])


def x_table(length, devices):
    width = length // 2 // devices
    points = np.arange(length)
    base = turn(width * np.arange(devices), points, length)
    step = turn(np.arange(width), points, length)
    table = outer_cosine(base, np.concatenate([step, step + math.pi / 2]))
    rows = lax.broadcasted_iota(jnp.int32, table.shape, 0)
    odd = lax.broadcasted_iota(jnp.int32, table.shape, 1) % 2
    return jnp.where(rows == width, 1.0 - 2.0 * odd.astype(jnp.float32), table)


def y_table(length):
    freq = np.arange(length).reshape(-1, 1, LANES)
    freq = np.broadcast_to(freq, (length // LANES, 2, LANES)).reshape(-1)
    shift = np.broadcast_to(np.array([0.0, math.pi / 2])[None, :, None], (length // LANES, 2, LANES)).reshape(-1)
    fine = 32
    coarse = turn(fine * np.arange(length // fine), freq, length) - shift[None]
    return outer_cosine(coarse, turn(np.arange(fine), freq, length))


def plane(wave_x, wave_y):
    square = wave_x * wave_x + wave_y * wave_y
    anchor = square == 0.0
    norm = jnp.sqrt(jnp.where(anchor, 1.0, square))
    unit_x = jnp.where(anchor, 0.0, wave_x / norm)
    unit_y = jnp.where(anchor, 0.0, wave_y / norm)
    depth = THICKNESS * norm
    series = 1.0 - depth / 11.0
    for term in range(10, 2, -1):
        series = 1.0 - depth / term * series
    rest = jnp.where(depth < 0.5, 0.5 * depth * series, 1.0 - (1.0 - jnp.exp(-depth)) / depth)
    rest = jnp.where(anchor, 0.0, rest)
    self_z = 1.0 - rest
    form = jnp.where(anchor, 0.0, 0.5 * depth * self_z * self_z)
    near = form * jnp.exp(-norm * (LAYER_PITCH - THICKNESS))
    decay = jnp.exp(-norm * LAYER_PITCH)
    laplace = 2.0 * jnp.cos(wave_x) + 2.0 * jnp.cos(wave_y) - 4.0
    return unit_x, unit_y, rest, self_z, near, decay, laplace


def field_of(spectra, factors, sign_x, sign_y, params, layers):
    unit_x, unit_y, rest, self_z, near, decay, laplace = factors
    unit_x = unit_x * sign_x
    unit_y = unit_y * sign_y
    along, normal, up, down = [], [], [], []
    for l in range(layers):
        moment = params[l, 0]
        along.append([moment * (unit_x * spectra[l][0][i] + unit_y * spectra[l][1][i]) for i in range(2)])
        normal.append([moment * spectra[l][2][i] for i in range(2)])
    zero = jnp.zeros_like(along[0][0])
    carry = [zero, zero]
    for l in range(layers):
        up.append(carry)
        carry = [
            along[l][0] + normal[l][1] + decay * carry[0],
            along[l][1] - normal[l][0] + decay * carry[1],
        ]
    carry = [zero, zero]
    for l in reversed(range(layers)):
        down.append(carry)
        carry = [
            along[l][0] - normal[l][1] + decay * carry[0],
            along[l][1] + normal[l][0] + decay * carry[1],
        ]
    down = down[::-1]
    out = []
    for l in range(layers):
        psi = [rest * along[l][i] + near * (up[l][i] + down[l][i]) for i in range(2)]
        chi = [
            self_z * normal[l][0] - near * (up[l][1] - down[l][1]),
            self_z * normal[l][1] + near * (up[l][0] - down[l][0]),
        ]
        stiff = params[l, 1] * laplace
        below = RKKY_STRENGTH * params[l, 2]
        above = RKKY_STRENGTH * params[l, 3]
        comps = []
        for c in range(3):
            pair = []
            for i in range(2):
                value = -(unit_x * psi[i] if c == 0 else unit_y * psi[i] if c == 1 else chi[i])
                value = value + stiff * spectra[l][c][i]
                if l > 0:
                    value = value + below * spectra[l - 1][c][i]
                if l < layers - 1:
                    value = value + above * spectra[l + 1][c][i]
                pair.append(value)
            comps.append(pair)
        out.append(comps)
    return out


def spectral_kernel(layers, width, nx, ny, at_ref, params_ref, in_ref, out_ref):
    device = at_ref[0]
    block = pl.program_id(0)
    scale = 1.0 / (nx * ny)
    low, high = pl.ds(0, LANES), pl.ds(LANES, LANES)
    real, imag = pl.ds(0, width), pl.ds(width, width)

    def wave_y(shape):
        place = block * LANES + lax.broadcasted_iota(jnp.int32, shape, len(shape) - 1)
        nyquist = place == ny // 2
        signed = jnp.where(place < ny // 2, place, place - ny)
        return nyquist, 2.0 * math.pi / ny * signed.astype(jnp.float32)

    shape = (width, LANES)
    column = device * width + lax.broadcasted_iota(jnp.int32, shape, 0)
    generic = jnp.where(column == 0, 0.0, 1.0)
    weight = scale * (1.0 + generic)
    nyquist, rows_y = wave_y(shape)
    factors = plane(2.0 * math.pi / nx * column.astype(jnp.float32), rows_y)
    has_nyquist = block == ny // 2 // LANES

    def load():
        spectra = []
        for l in range(layers):
            comps = []
            for c in range(3):
                at = 3 * l + c
                comps.append(
                    [
                        in_ref[at, real, low] + generic * in_ref[at, imag, high],
                        generic * in_ref[at, imag, low] - in_ref[at, real, high],
                    ]
                )
            spectra.append(comps)
        return spectra

    def store(field):
        for l in range(layers):
            for c in range(3):
                at = 3 * l + c
                field_real = weight * field[l][c][0]
                field_imag = weight * field[l][c][1]
                out_ref[at, real, low] = field_real
                out_ref[at, real, high] = -field_imag
                out_ref[at, imag, low] = field_imag
                out_ref[at, imag, high] = field_real

    def mean_of(one, two):
        return [[[0.5 * (a + b) for a, b in zip(p, q)] for p, q in zip(u, v)] for u, v in zip(one, two)]

    @pl.when(jnp.logical_not(has_nyquist))
    def _():
        store(field_of(load(), factors, 1.0, 1.0, params_ref, layers))

    @pl.when(has_nyquist)
    def _():
        spectra = load()
        flip = jnp.where(nyquist, -1.0, 1.0)
        store(
            mean_of(
                field_of(spectra, factors, 1.0, 1.0, params_ref, layers),
                field_of(spectra, factors, 1.0, flip, params_ref, layers),
            )
        )

    @pl.when(device == 0)
    def _():
        line = (1, LANES)
        corner, line_y = wave_y(line)
        line_factors = plane(jnp.full(line, -math.pi, jnp.float32), line_y)
        row = pl.ds(width, 1)
        spectra = [
            [[in_ref[3 * l + c, row, low], -in_ref[3 * l + c, row, high]] for c in range(3)]
            for l in range(layers)
        ]
        flip = jnp.where(corner, -1.0, 1.0)
        field = mean_of(
            field_of(spectra, line_factors, 1.0, 1.0, params_ref, layers),
            field_of(spectra, line_factors, -1.0, flip, params_ref, layers),
        )
        for l in range(layers):
            for c in range(3):
                out_ref[3 * l + c, row, low] = scale * field[l][c][0]
                out_ref[3 * l + c, row, high] = -scale * field[l][c][1]


def spectral_field(spectra, params, device, nx, ny):
    layers = params.shape[0]
    lead, pair, length = spectra.shape
    block = (lead, pair, 2 * LANES)
    return pl.pallas_call(
        functools.partial(spectral_kernel, layers, pair // 2, nx, ny),
        out_shape=jax.ShapeDtypeStruct(spectra.shape, jnp.float32),
        grid=(length // (2 * LANES),),
        in_specs=[
            pl.BlockSpec(memory_space=pltpu.SMEM),
            pl.BlockSpec(memory_space=pltpu.SMEM),
            pl.BlockSpec(block, lambda i: (0, 0, i)),
        ],
        out_specs=pl.BlockSpec(block, lambda i: (0, 0, i)),
        cost_estimate=pl.CostEstimate(flops=60 * spectra.size, bytes_accessed=8 * spectra.size, transcendentals=0),
        name="spectral_field",
    )(device, params, spectra)


def cross_product(one, two):
    return [
        one[1] * two[2] - one[2] * two[1],
        one[2] * two[0] - one[0] * two[2],
        one[0] * two[1] - one[1] * two[0],
    ]


def on_device(magnet, saturation, stiffness, damping, interface_sign):
    axes = ("layer", "row")
    layers, bands = lax.axis_size("layer"), lax.axis_size("row")
    devices = layers * bands
    rows, nx = magnet.shape[2], magnet.shape[3]
    ny = rows * bands
    pair = nx // devices
    own = jnp.concatenate(
        [saturation[:, None], stiffness[:, None], interface_sign.astype(jnp.float32)], axis=1
    )
    params = lax.all_gather(own, "layer", axis=0, tiled=True)
    device = (lax.axis_index("layer") * bands + lax.axis_index("row")).reshape(1)
    flat = magnet.reshape(3 * rows, nx)
    table_x = x_table(nx, devices)
    table_y = y_table(ny)
    half = lax.dot_general(table_x, flat, (((1,), (1,)), ((), ())), precision=HIGH)
    sent = half.reshape(devices, pair, 3 * rows)
    got = lax.all_to_all(sent, axes, split_axis=0, concat_axis=0, tiled=True)
    got = got.reshape(layers, bands, pair, 3, rows).transpose(0, 3, 2, 1, 4)
    got = got.reshape(layers * 3 * pair, ny)
    spectra = lax.dot_general(got, table_y, (((1,), (0,)), ((), ())), precision=HIGH)
    field = spectral_field(spectra.reshape(layers * 3, pair, 2 * ny), params, device, nx, ny)
    back = lax.dot_general(
        field.reshape(layers * 3 * pair, 2 * ny), table_y, (((1,), (1,)), ((), ())), precision=HIGH
    )
    back = back.reshape(layers, 3, pair, bands, rows).transpose(0, 3, 2, 1, 4)
    back = back.reshape(devices, pair, 3 * rows)
    home = lax.all_to_all(back, axes, split_axis=0, concat_axis=0, tiled=True)
    total = lax.dot_general(
        home.reshape(nx, 3 * rows), table_x, (((0,), (0,)), ((), ())), precision=HIGH
    )
    total = total.reshape(3, rows, nx)
    spin = magnet.reshape(3, rows, nx)
    precess = cross_product(spin, total)
    relax = cross_product(spin, precess)
    damp = damping[0]
    factor = -1.0 / (1.0 + damp * damp)
    torque = jnp.stack([factor * (p + damp * q) for p, q in zip(precess, relax)])
    return torque.reshape(magnet.shape)


def solution(mesh):
    in_specs = (P(None, "layer", "row", None), P("layer"), P("layer"), P("layer"), P("layer", None))
    out_specs = P(None, "layer", "row", None)
    return jax.shard_map(
        on_device, mesh=mesh, in_specs=in_specs, out_specs=out_specs, check_vma=False
    )
```

time: 696 us -> 233 us (0.33)
  waiting for transfers between devices: 351 us -> 108 us
  matrix products: 150 us -> 46.1 us
  local copies, waits for them, and re-layouts: 112 us -> 21.2 us
  other arithmetic: 38.5 us -> 9.28 us
  blocking collectives: 0 us -> 21.1 us
  starting transfers between devices: 31.6 us -> 12.7 us
  Pallas kernels: 0 us -> 9.09 us
    all_to_all x4 -> x2, waiting for transfers between devices: 351 us -> 108 us  [the longest x1 67.6 us: on_device(): home = lax.all_to_all(back, axes, split_axis=0, concat_axis=0, tiled=True)]
    dot_general x30 -> x4, matrix products: 150 us -> 46.1 us  [the longest x1 15.1 us: on_device(): lax.dot_general(got, table_y, (((1,), (0,)), ((), ())), precision=HIGH)]
    slice x11 -> x0, local copies, waits for them, and re-layouts: 31.2 us -> none  [the longest x1 11.7 us: forward_y(): halves[:, :, :, 0]]
    div x3 -> x0, local copies, waits for them, and re-layouts: 27.4 us -> none  [the longest x2 22.8 us: inverse_y(): filled = jnp.stack([real_out, imag_out], axis=3) / length]
    all_gather x0 -> x1, blocking collectives: none -> 21.1 us  [on_device(): params = lax.all_gather(own, 'layer', axis=0, tiled=True)]
    all_to_all x3 -> x0, local copies, waits for them, and re-layouts: 19.4 us -> none  [the longest x2 12.8 us: on_device(): lax.all_to_all(inverse_y(field_spectra), 'row', split_axis=2, concat_axis...]
    dot_general x1 -> x0, other arithmetic: 12.2 us -> none  [contract(): return jnp.einsum('tmyx,myx->tyx', weight, values, precision=HIGHEST)]
    another operation x3 -> x0, local copies, waits for them, and re-layouts: 11.5 us -> none
  transfers between devices with their start and end apart: 8 -> 2, of which waited for: 4 -> 2; matrix products, arithmetic and copies ran while one was open for 9% -> 2% of each run, Pallas kernels for 0% -> 0%
where the time goes in v1:
time: 233 us; the launch traced here: 229 us
  waiting for transfers between devices  108 us (46%)
  matrix products  46.1 us (20%)
  local copies, waits for them, and re-layouts  21.2 us (9%)
  blocking collectives  21.1 us (9%)
  starting transfers between devices  12.7 us (5%)
  other arithmetic  9.28 us (4%)
  Pallas kernels  9.09 us (4%)
    all_to_all x1, waiting for transfers between devices, on_device(): home = lax.all_to_all(back, axes, split_axis=0, concat_axis=0, tiled=True)  67.6 us
    all_to_all x1, waiting for transfers between devices, on_device(): got = lax.all_to_all(sent, axes, split_axis=0, concat_axis=0, tiled=True)  40.2 us
    all_gather x1, blocking collectives, on_device(): params = lax.all_gather(own, 'layer', axis=0, tiled=True)  21.1 us
    dot_general x1, matrix products, on_device(): lax.dot_general(got, table_y, (((1,), (0,)), ((), ())), precision=HIGH)  15.1 us
    dot_general x1, matrix products, on_device(): lax.dot_general(field.reshape(layers * 3 * pair, 2 * ny), table_y, (((1,)...  13.7 us
    dot_general x1, matrix products, on_device(): lax.dot_general(table_x, flat, (((1,), (1,)), ((), ())), precision=HIGH)  9.46 us
    pallas_call x1, Pallas kernels, spectral_field(): pl.pallas_call(functools.partial(spectral_kernel, layers, pair // 2, nx,...  9.09 us
    dot_general x1, matrix products, on_device(): lax.dot_general(home.reshape(nx, 3 * rows), table_x, (((0,), (0,)), ((),...  7.84 us
  transfers between devices with their start and end apart: 2, of which 2 were waited for; matrix products, arithmetic and copies ran while one was open for 2% of the time, Pallas kernels for 0%

profile of v1, /device:TPU:2, one launch (start us, length us, event | category | flops | bytes accessed | tf_op | source)
XLA Modules:
  0.0 229.3 jit_solution(3207910200272407902)
XLA Ops:
  0.0 9.5 %fusion.1 = f32[32,32,768]{2,1,0:T(8,128)} fusion(f32[768,1024,1]{1,0,2:T(8,128)} %bitcast.120, f32[32,1024]{1,0:T(8,128)} %constant.56.clone, f32[32,1024]{1,0:T(8,128)} %constant.68, f32[32,1024]{1,0:T(8,128)} %constant.54.clone, f32[32,1024]{1,0:T(8,128)} %constant.67, s32[1024]{0:T(1024)S(1)} %get-tuple-element.11, s32[1024]{0:T(1024)S(1)} %get-tuple-element.12, ...), kind=kOutput, calls=%fused_computation.3 | convolution fusion | flops 4840226816 | bytes 6825984 | tf_op jit(solution)/shard_map/dot_general | solution.py:253
  9.5 0.0 copy-start.2
  9.5 0.0 copy-start.1
  9.5 6.1 %all-to-all-start = ((f32[32,32,768]{2,1,0:T(8,128)}), f32[32,32,768]{2,1,0:T(8,128)S(1)}, u32[]{:S(2)}, u32[]{:S(2)}) async-start(f32[32,32,768]{2,1,0:T(8,128)} %fusion.1), calls=%async_computation | async-start | bytes 6291456 | tf_op jit(solution)/shard_map/all_to_all | solution.py:255
  16.9 0.0 copy-done.2
  16.9 0.1 maximum_bitcast_fusion.1
  17.0 21.1 %all-gather = f32[8,1,4]{2,1,0:T(1,128)} all-gather(f32[1,1,4]{2,1,0:T(1,128)S(1)} %maximum_bitcast_fusion.1), channel_id=1, replica_groups=mesh['layer'=8,'row'=4] {'layer'}, dimensions={0}, use_global_device_ids=true | all-gather | bytes 144 | tf_op jit(solution)/shard_map/all_gather | solution.py:248
  38.1 0.0 copy-done.1
  38.1 5.6 %multiply_subtract_fusion = f32[32,32,2048]{2,1,0:T(8,128)} fusion(f32[32,2048]{1,0:T(8,128)} %constant.60.clone, f32[32,2048]{1,0:T(8,128)} %constant.70, f32[32,2048]{1,0:T(8,128)S(1)} %copy-done.1, f32[32,2048]{1,0:T(8,128)} %constant.69), kind=kLoop, calls=%fused_computation | loop fusion | flops 6291456 | bytes 9437184 | tf_op jit(solution)/shard_map/sub | solution.py:30
  43.7 40.2 %all-to-all-done = f32[32,32,768]{2,1,0:T(8,128)S(1)} async-done(((f32[32,32,768]{2,1,0:T(8,128)}), f32[32,32,768]{2,1,0:T(8,128)S(1)}, u32[]{:S(2)}, u32[]{:S(2)}) %all-to-all-start) | async-done | bytes 3145760 | tf_op jit(solution)/shard_map/all_to_all | solution.py:255
  83.9 3.3 %reshape.145 = f32[8,4,32,3,256]{4,3,2,1,0:T(4,128)} reshape(f32[32,32,768]{2,1,0:T(8,128)S(1)} %all-to-all-done) | data formatting | bytes 6291456 | tf_op jit(solution)/shard_map/reshape | solution.py:256
  87.2 4.2 %copy.24 = f32[8,3,32,4,256]{4,3,2,1,0:T(4,128)S(1)} copy(f32[8,3,32,4,256]{4,1,2,3,0:T(4,128)} %bitcast.119) | data formatting | bytes 6291456 | tf_op jit(solution)/shard_map/transpose | solution.py:256
  91.4 3.0 %dot_general.17 = f32[24,32,1024]{2,1,0:T(8,128)} reshape(f32[8,3,32,4,256]{4,3,2,1,0:T(4,128)S(1)} %copy.24) | data formatting | bytes 6291456 | tf_op jit(solution)/shard_map/dot_general | solution.py:258
  94.5 15.1 %fusion.52.in_ref = f32[24,32,2048]{2,1,0:T(8,128)} fusion(f32[24,32,1024]{2,1,0:T(8,128)} %dot_general.17, f32[1024,2048,1]{1,0,2:T(8,128)} %bitcast.121), kind=kOutput, calls=%fused_computation.68 | convolution fusion | flops 9663676416 | bytes 17825792 | tf_op jit(solution)/shard_map/dot_general | solution.py:258
  109.6 9.1 %spectral_field.1 = f32[24,32,2048]{2,1,0:T(8,128)} custom-call(s32[1]{0:T(128)} %bitcast.2.at_ref, f32[8,4]{1,0:T(8,128)} %bitcast.124, f32[24,32,2048]{2,1,0:T(8,128)} %fusion.52.in_ref), custom_call_target="tpu_custom_call" | custom-call | flops 94371840 | bytes 12582912 | tf_op jit(solution)/shard_map/spectral_field/pallas_call | solution.py:215
  118.7 13.7 %convolution_bitcast_fusion = f32[8,4,32,3,256]{4,2,1,3,0:T(8,128)S(1)} fusion(f32[8,3,32,2048,1]{3,2,4,1,0:T(8,128)} %bitcast.123, f32[4,256,2048,1,1]{2,1,0,4,3:T(8,128)} %bitcast.122), kind=kOutput, calls=%fused_computation.26 | convolution fusion | flops 9663676416 | bytes 17825792 | tf_op jit(solution)/shard_map/dot_general | solution.py:260
  132.4 4.5 %copy.26 = f32[8,4,32,3,256]{4,3,2,1,0:T(4,128)} copy(f32[8,4,32,3,256]{4,2,1,3,0:T(8,128)S(1)} %convolution_bitcast_fusion) | data formatting | bytes 6291456 | tf_op jit(solution)/shard_map/transpose | solution.py:263
  136.9 6.0 %reshape.146 = f32[32,32,768]{2,1,0:T(8,128)} reshape(f32[8,4,32,3,256]{4,3,2,1,0:T(4,128)} %copy.26) | data formatting | bytes 6291456 | tf_op jit(solution)/shard_map/reshape | solution.py:264
  142.9 0.0 copy-start.3
  142.9 0.0 copy-start.4
  142.9 0.0 copy-start.5
  142.9 6.6 %all-to-all-start.1 = ((f32[32,32,768]{2,1,0:T(8,128)}), f32[32,32,768]{2,1,0:T(8,128)}, u32[]{:S(2)}, u32[]{:S(2)}) async-start(f32[32,32,768]{2,1,0:T(8,128)} %reshape.146), calls=%async_computation.1 | async-start | bytes 6291456 | tf_op jit(solution)/shard_map/all_to_all | solution.py:265
  150.2 0.0 copy-start
  150.2 67.6 %all-to-all-done.1 = f32[32,32,768]{2,1,0:T(8,128)} async-done(((f32[32,32,768]{2,1,0:T(8,128)}), f32[32,32,768]{2,1,0:T(8,128)}, u32[]{:S(2)}, u32[]{:S(2)}) %all-to-all-start.1) | async-done | bytes 3145760 | tf_op jit(solution)/shard_map/all_to_all | solution.py:265
  217.9 0.0 copy-done.3
  217.9 0.0 copy-done.4
  217.9 0.0 copy-done.5
  217.9 7.8 %fusion.22 = f32[768,1024]{1,0:T(8,128)S(1)} fusion(f32[32,32,768]{2,1,0:T(8,128)} %all-to-all-done.1, f32[32,1024]{1,0:T(8,128)S(1)} %copy-done.4, f32[32,1024]{1,0:T(8,128)} %constant.68, f32[32,1024]{1,0:T(8,128)S(1)} %copy-done.3, f32[32,1024]{1,0:T(8,128)S(1)} %copy-done.5, s32[1024]{0:T(1024)S(1)} %get-tuple-element.11, ...), kind=kOutput, calls=%fused_computation.25 | convolution fusion | flops 4840226816 | bytes 6825984 | tf_op jit(solution)/shard_map/dot_general | solution.py:266
  225.7 0.0 copy-done
  225.7 0.9 fusion.40
  226.6 0.8 fusion.29
  227.4 1.9 maximum_bitcast_fusion
  (4 shorter events, 0.0 us)
Async XLA Ops:
  9.5 7.4 %copy-start.2 = (s32[1,2]{1,0:T(1,128)S(1)}, s32[1,2]{1,0:T(1,128)}, u32[]{:S(2)}) copy-start(s32[1,2]{1,0:T(1,128)} %param.17) | copy-start | bytes 28
  9.5 28.6 %copy-start.1 = (f32[32,2048]{1,0:T(8,128)S(1)}, f32[32,2048]{1,0:T(8,128)}, u32[]{:S(2)}) copy-start(f32[32,2048]{1,0:T(8,128)} %constant.58.clone) | copy-start | bytes 786436
  9.5 74.4 %all-to-all-start = ((f32[32,32,768]{2,1,0:T(8,128)}), f32[32,32,768]{2,1,0:T(8,128)S(1)}, u32[]{:S(2)}, u32[]{:S(2)}) async-start(f32[32,32,768]{2,1,0:T(8,128)} %fusion.1), calls=%async_computation | async-start | bytes 6291456 | tf_op jit(solution)/shard_map/all_to_all | solution.py:255
  142.9 74.9 %copy-start.3 = (f32[32,1024]{1,0:T(8,128)S(1)}, f32[32,1024]{1,0:T(8,128)}, u32[]{:S(2)}) copy-start(f32[32,1024]{1,0:T(8,128)} %constant.54.clone) | copy-start | bytes 393220
  142.9 74.9 %copy-start.4 = (f32[32,1024]{1,0:T(8,128)S(1)}, f32[32,1024]{1,0:T(8,128)}, u32[]{:S(2)}) copy-start(f32[32,1024]{1,0:T(8,128)} %constant.56.clone) | copy-start | bytes 393220
  142.9 74.9 %copy-start.5 = (f32[32,1024]{1,0:T(8,128)S(1)}, f32[32,1024]{1,0:T(8,128)}, u32[]{:S(2)}) copy-start(f32[32,1024]{1,0:T(8,128)} %constant.67) | copy-start | bytes 393220
  142.9 74.9 %all-to-all-start.1 = ((f32[32,32,768]{2,1,0:T(8,128)}), f32[32,32,768]{2,1,0:T(8,128)}, u32[]{:S(2)}, u32[]{:S(2)}) async-start(f32[32,32,768]{2,1,0:T(8,128)} %reshape.146), calls=%async_computation.1 | async-start | bytes 6291456 | tf_op jit(solution)/shard_map/all_to_all | solution.py:265
  150.2 75.5 %copy-start = (f32[3,1,256,1024]{3,2,1,0:T(8,128)S(1)}, f32[3,1,256,1024]{3,2,1,0:T(8,128)}, u32[]{:S(2)}) copy-start(f32[3,1,256,1024]{3,2,1,0:T(8,128)} %param.13) | copy-start | bytes 9437188
